TPU v7x, 32 devices: a whole 2x2x4 slice. The times are simulated.
32 devices in a mesh: mem: 8 (over y, x, core), sub: 4 (over z).
Axes of the slice: x: 2, y: 2, z: 4, core: 2. Of those that a mesh axis runs over, the one named last changes fastest.
Arguments:
- control: bfloat16 [64, 1024, 128], P('mem', 'sub'), may hold values from -6 to 6
- perturb: bfloat16 [64, 1024, 128], P('mem', 'sub'), may hold values from -6 to 6
- obs_column: int32 [8, 4, 1024], P('mem', 'sub'), may hold values from 0 to 255
- obs_count: int32 [8, 4], P('mem', 'sub'), may hold values from 128 to 1024, as said below
- obs_background: bfloat16 [8, 4, 1024, 128], P('mem', 'sub'), may hold values from -6 to 6
- obs_value: bfloat16 [8, 4, 1024, 128], P('mem', 'sub'), may hold values from -6 to 6
- obs_weight: float32 [8, 4, 1024], P('mem', 'sub'), may hold values from 0.05 to 0.5
- w_in: bfloat16 [128, 2048], replicated, may hold values from -0.5 to 0.5
- b_in: float32 [2048], replicated, may hold values from -3 to 3
- w_out: bfloat16 [2048, 128], replicated, may hold values from -0.125 to 0.125
Outputs:
- increment: float32 [1024, 128], P(('sub', 'mem'))
- grad_columns: float32 [1024, 128], P(('sub', 'mem'))
Inputs may be any that keep to these rules, and one draw needn't show every extreme that they name: `obs_count`: at least one batch has all 1024 slots live in every draw.
All inputs are finite; a program needn't handle non-finite values.
Results may differ from a plain program's by a relative error of at most 0.0025.
Values sent between devices are 32-bit elements; how exact they have to be, the bound alone decides.
No kernel may reach another device: no remote copies, remote signals or barrier semaphores. Data moves between devices by JAX's collectives and lax.ppermute only.
A program may use at most 64 MiB of HBM per device.

v0:
```python
import jax
import jax.numpy as jnp
from jax import lax
from jax.sharding import PartitionSpec as P

SWEEPS = 4
diffusion = 0.4


def padded_2(block, sides, width):
    for axis, dim in sides:
        count = lax.axis_size(axis)
        forward = [(i, i + 1) for i in range(count - 1)]
        forward.append((count - 1, 0))
        backward = [(target, source) for source, target in forward]
        low = lax.ppermute(
            lax.slice_in_dim(block, block.shape[dim] - width, None, axis=dim), axis, forward
        )
        high = lax.ppermute(lax.slice_in_dim(block, 0, width, axis=dim), axis, backward)
        block = jnp.concatenate([low, block, high], axis=dim)
    return block


def gelu_tanh(values):
    return jax.nn.gelu(values, approximate=True)


def sweep(padded):
    middle = padded[:, 1:-1]
    return middle + diffusion * (padded[:, :-2] - 2.0 * middle + padded[:, 2:])


def observe_block(whole_cols, indices, live, background, targets, weights, w_in, b_in, w_out):
    sampled = jnp.take(whole_cols, indices, axis=0)
    inputs = (background.astype(jnp.float32) + sampled).astype(jnp.bfloat16)
    hidden_pre = jnp.dot(inputs, w_in, preferred_element_type=jnp.float32) + b_in
    hidden, pullback = jax.vjp(gelu_tanh, hidden_pre)
    hidden_low = hidden.astype(jnp.bfloat16)
    outputs = jnp.dot(hidden_low, w_out, preferred_element_type=jnp.float32)
    misfit = ((outputs - targets.astype(jnp.float32)) * (weights * live)[:, None]).astype(
        jnp.bfloat16
    )
    back_hidden = lax.dot_general(
        misfit, w_out, (((1,), (1,)), ((), ())), preferred_element_type=jnp.float32
    )
    (back_pre,) = pullback(back_hidden)
    back_pre = back_pre.astype(jnp.bfloat16)
    back_input = lax.dot_general(
        back_pre, w_in, (((1,), (1,)), ((), ())), preferred_element_type=jnp.float32
    )
    back_input = back_input.astype(jnp.bfloat16)
    column_ids = lax.broadcasted_iota(jnp.int32, (indices.shape[0], whole_cols.shape[0]), 1)
    one_hot = (indices[:, None] == column_ids).astype(jnp.bfloat16)
    return lax.dot_general(
        one_hot, back_input, (((0,), (0,)), ((), ())), preferred_element_type=jnp.float32
    )


def per_device(
    control,
    perturb,
    obs_column,
    obs_count,
    obs_background,
    obs_value,
    obs_weight,
    w_in,
    b_in,
    w_out,
):
    field = control.astype(jnp.float32)
    padded = padded_2(field, (("sub", 1),), SWEEPS)
    for sweep_index in range(SWEEPS):
        padded = sweep(padded)
    field = padded
    partial_sum = jnp.sum(field * perturb.astype(jnp.float32), axis=0)
    members = perturb.shape[0] * lax.axis_size("mem")
    scale = (members - 1) ** (-0.5)
    owned = partial_sum.shape[0] // lax.axis_size("mem")
    whole_cols = lax.psum(partial_sum, "mem") * scale
    increment = lax.dynamic_slice_in_dim(whole_cols, lax.axis_index("mem") * owned, owned, 0)
    indices = obs_column.reshape(-1)
    background = obs_background.reshape(indices.shape[0], -1)
    targets = obs_value.reshape(indices.shape[0], -1)
    weights = obs_weight.reshape(-1)
    live_count = obs_count.reshape(())
    slot_ids = lax.broadcasted_iota(jnp.int32, (indices.shape[0],), 0)
    live = (slot_ids < live_count).astype(jnp.float32)
    gradient = observe_block(
        whole_cols, indices, live, background, targets, weights, w_in, b_in, w_out
    )
    grad_columns = lax.psum_scatter(gradient, "mem", scatter_dimension=0, tiled=True)
    return (increment, grad_columns)


def solution(mesh):
    return jax.shard_map(
        per_device,
        mesh=mesh,
        in_specs=(
            P("mem", "sub", None),
            P("mem", "sub", None),
            P("mem", "sub", None),
            P("mem", "sub"),
            P("mem", "sub", None, None),
            P("mem", "sub", None, None),
            P("mem", "sub", None),
            P(),
            P(),
            P(),
        ),
        out_specs=(P(("sub", "mem"), None), P(("sub", "mem"), None)),
        check_vma=False,
    )
```

profile of v0, /device:TPU:0, one launch (start us, length us, event | category | flops | bytes accessed | tf_op | source)
XLA Modules:
  0.0 135.8 jit_solution(15653344673557643430)
XLA Ops:
  7.2 0.0 copy-start
  7.2 0.0 all-reduce.2.cloned.1.call-start
  7.2 0.8 fusion.48
  8.0 5.1 %collective-permute-start.1 = (f32[8,4,128]{2,1,0:T(4,128)S(1)}, f32[8,4,128]{2,1,0:T(4,128)S(1)}, u32[]{:S(2)}, u32[]{:S(2)}) collective-permute-start(f32[8,4,128]{2,1,0:T(4,128)S(1)} %get-tuple-element.3), channel_id=1, source_target_pairs={{1,0},{2,1},{3,2},{0,3},{5,4},{6,5},{7,6},{4,7},{9,8},{10,9},{11,1... | collective-permute-start | bytes 49160 | tf_op jit(solution)/shard_map/ppermute | solution.py:19
  13.2 0.0 collective-permute-start
  13.2 0.7 compare_select_fusion
  14.5 0.7 fusion.36
  15.2 1.1 convert_element_type.35
  16.3 2.4 %collective-permute-done = f32[8,4,128]{2,1,0:T(4,128)S(1)} collective-permute-done((f32[8,4,128]{2,1,0:T(4,128)S(1)}, f32[8,4,128]{2,1,0:T(4,128)S(1)}, u32[]{:S(2)}, u32[]{:S(2)}) %collective-permute-start) | collective-permute-done | bytes 16416 | tf_op jit(solution)/shard_map/ppermute | solution.py:16
  18.7 0.1 pad_maximum_fusion
  18.8 0.0 copy-start.4
  18.8 0.3 fusion.23
  19.1 0.0 copy-start.2
  19.1 0.3 fusion.21
  19.5 0.3 fusion.19
  19.8 1.1 fusion.27
  20.9 0.0 all-reduce.2.cloned.1.call-update
  20.9 0.0 reduce-scatter.2.cloned.1.call-start
  21.0 52.6 %all-reduce.2.cloned.1.call-done = f32[256,128]{1,0:T(8,128)} async-done(((f32[256,128]{1,0:T(8,128)}), f32[256,128]{1,0:T(8,128)}) %all-reduce.2.cloned.1.call-update) | async-done | bytes 131088 | tf_op jit(solution)/shard_map/psum | solution.py:80
  73.6 0.9 broadcast_multiply_fusion
  74.5 0.0 copy-start.5
  74.5 0.0 copy-start.6
  74.5 0.0 copy-start.7
  74.5 2.8 %gather_fusion = f32[1024,128]{1,0:T(8,128)S(1)} fusion(f32[256,128]{1,0:T(8,128)S(1)} %broadcast_multiply_fusion, s32[1024]{0:T(1024)S(1)} %broadcast_clamp_fusion), kind=kCustom, calls=%fused_computation | custom fusion | bytes 1052672 | tf_op jit(solution)/shard_map/jit(_take)/gather | solution.py:34
  77.4 1.3 fusion.31
  78.7 3.2 %copy-done.1 = f32[1024,2048]{1,0:T(8,128)} copy-done((f32[1024,2048]{1,0:T(8,128)}, f32[1024,2048]{1,0:T(8,128)S(1)}, u32[]{:S(2)}) %copy-start.1) | copy-done | bytes 8388632
  81.9 3.2 %fusion.14 = bf16[1024,128]{1,0:T(8,128)(2,1)S(1)} fusion(bf16[2048,128]{1,0:T(8,128)(2,1)S(1)} %copy-done.5, f32[1024,2048]{1,0:T(8,128)S(1)} %fusion.31, f32[2048]{0:T(1024)S(1)} %copy-done.7, bf16[1,1,1024,128]{3,2,1,0:T(8,128)(2,1)S(1)} %copy-done.6, f32[1024]{0:T(1024)S(1)} %fusion.36), kind=kOutput, calls=%fused_computation.16 | convolution fusion | flops 558366720 | bytes 9449472 | tf_op jit(solution)/shard_map/dot_general | solution.py:39
  85.1 9.4 %fusion.15 = bf16[1024,128]{1,0:T(8,128)(2,1)S(1)} fusion(bf16[128,2048]{1,0:T(8,128)(2,1)S(1)} %copy-done, f32[1024,2048]{1,0:T(8,128)} %copy-done.1, f32[2048]{0:T(1024)S(1)} %copy-done.7, bf16[1024,128]{1,0:T(8,128)(2,1)S(1)} %fusion.14, bf16[2048,128]{1,0:T(8,128)(2,1)S(1)} %copy-done.5), kind=kOutput, calls=%fused_computation.17 | convolution fusion | flops 1117913088 | bytes 9969664 | tf_op jit(solution)/shard_map/dot_general | solution.py:48
  94.6 1.3 fusion.28
  95.8 0.0 reduce-scatter.2.cloned.1.call-update
  95.9 0.6 constant_dynamic-slice_fusion
  96.5 32.5 %reduce-scatter.2.cloned.1.call-done = f32[32,128]{1,0:T(8,128)} async-done(((f32[256,128]{1,0:T(8,128)}), f32[32,128]{1,0:T(8,128)}) %reduce-scatter.2.cloned.1.call-update) | async-done | bytes 16400 | tf_op jit(solution)/shard_map/reduce_scatter | solution.py:92
  (12 shorter events, 0.0 us)
Async XLA Ops:
  7.2 70.2 %copy-start = (bf16[128,2048]{1,0:T(8,128)(2,1)S(1)}, bf16[128,2048]{1,0:T(8,128)(2,1)}, u32[]{:S(2)}) copy-start(bf16[128,2048]{1,0:T(8,128)(2,1)} %param.17) | copy-start | bytes 1572868
  7.2 66.4 %all-reduce.2.cloned.1.call-start = ((), (), s32[]{:S(2)}) async-start(), calls=%async_computation.1 | async-start | bytes 262144 | tf_op jit(solution)/shard_map/psum | solution.py:80
  8.0 11.8 %copy-start.3 = (bf16[8,256,128]{2,1,0:T(8,128)(2,1)S(1)}, bf16[8,256,128]{2,1,0:T(8,128)(2,1)}, u32[]{:S(2)}) copy-start(bf16[8,256,128]{2,1,0:T(8,128)(2,1)} %param.11) | copy-start | bytes 1572868
  8.0 8.3 %collective-permute-start.1 = (f32[8,4,128]{2,1,0:T(4,128)S(1)}, f32[8,4,128]{2,1,0:T(4,128)S(1)}, u32[]{:S(2)}, u32[]{:S(2)}) collective-permute-start(f32[8,4,128]{2,1,0:T(4,128)S(1)} %get-tuple-element.3), channel_id=1, source_target_pairs={{1,0},{2,1},{3,2},{0,3},{5,4},{6,5},{7,6},{4,7},{9,8},{10,9},{11,1... | collective-permute-start | bytes 49160 | tf_op jit(solution)/shard_map/ppermute | solution.py:19
  13.2 5.5 %collective-permute-start = (f32[8,4,128]{2,1,0:T(4,128)S(1)}, f32[8,4,128]{2,1,0:T(4,128)S(1)}, u32[]{:S(2)}, u32[]{:S(2)}) collective-permute-start(f32[8,4,128]{2,1,0:T(4,128)S(1)} %get-tuple-element.2), channel_id=1, source_target_pairs={{0,1},{1,2},{2,3},{3,0},{4,5},{5,6},{6,7},{7,4},{8,9},{9,10},{10,1... | collective-permute-start | bytes 49160 | tf_op jit(solution)/shard_map/ppermute | solution.py:16
  18.8 2.2 %copy-start.4 = (s32[1,1,1024]{2,1,0:T(1,128)S(1)}, s32[1,1,1024]{2,1,0:T(1,128)}, u32[]{:S(2)}) copy-start(s32[1,1,1024]{2,1,0:T(1,128)} %param.12) | copy-start | bytes 12292
  19.1 58.3 %copy-start.2 = (bf16[1,1,1024,128]{3,2,1,0:T(8,128)(2,1)S(1)}, bf16[1,1,1024,128]{3,2,1,0:T(8,128)(2,1)}, u32[]{:S(2)}) copy-start(bf16[1,1,1024,128]{3,2,1,0:T(8,128)(2,1)} %param.14) | copy-start | bytes 786436
  20.9 108.1 %reduce-scatter.2.cloned.1.call-start = ((), (), s32[]{:S(2)}) async-start(), calls=%async_computation.2 | async-start | bytes 147456 | tf_op jit(solution)/shard_map/reduce_scatter | solution.py:92
  74.5 7.4 %copy-start.5 = (bf16[2048,128]{1,0:T(8,128)(2,1)S(1)}, bf16[2048,128]{1,0:T(8,128)(2,1)}, u32[]{:S(2)}) copy-start(bf16[2048,128]{1,0:T(8,128)(2,1)} %param.19) | copy-start | bytes 1572868
  74.5 7.4 %copy-start.6 = (bf16[1,1,1024,128]{3,2,1,0:T(8,128)(2,1)S(1)}, bf16[1,1,1024,128]{3,2,1,0:T(8,128)(2,1)}, u32[]{:S(2)}) copy-start(bf16[1,1,1024,128]{3,2,1,0:T(8,128)(2,1)} %param.15) | copy-start | bytes 786436
  74.5 7.4 %copy-start.7 = (f32[2048]{0:T(1024)S(1)}, f32[2048]{0:T(1024)}, u32[]{:S(2)}) copy-start(f32[2048]{0:T(1024)} %param.18) | copy-start | bytes 24580
  78.7 3.2 %copy-start.1 = (f32[1024,2048]{1,0:T(8,128)}, f32[1024,2048]{1,0:T(8,128)S(1)}, u32[]{:S(2)}) copy-start(f32[1024,2048]{1,0:T(8,128)S(1)} %fusion.31) | copy-start | bytes 25165828
Sparse Core Ops, SparseCore 0:
  21.0 52.5 all-reduce.1
  96.0 32.9 reduce-scatter.1
where the time goes:
time: 136 us
  waiting for transfers between devices  87.5 us (64%)
  matrix products  15.2 us (11%)
  between operations  14.8 us (11%)
  local copies, waits for them, and re-layouts  7.49 us (6%)
  other arithmetic  5.53 us (4%)
  starting transfers between devices  5.21 us (4%)
    psum x1, waiting for transfers between devices, per_device(): whole_cols = lax.psum(partial_sum, 'mem') * scale  52.6 us
    reduce_scatter x1, waiting for transfers between devices, per_device(): lax.psum_scatter(gradient, 'mem', scatter_dimension=0, tiled=True)  32.5 us
    dot_general x1, matrix products, observe_block(): lax.dot_general(back_pre, w_in, (((1,), (1,)), ((), ())), preferred_eleme...  9.44 us
    ppermute x1, starting transfers between devices, padded_2(): lax.ppermute(lax.slice_in_dim(block, 0, width, axis=dim), axis, backward)  5.13 us
    unnamed x16, local copies, waits for them, and re-layouts  3.27 us
    dot_general x1, matrix products, observe_block(): outputs = jnp.dot(hidden_low, w_out, preferred_element_type=jnp.float32)  3.19 us
    gather x1, local copies, waits for them, and re-layouts, observe_block(): sampled = jnp.take(whole_cols, indices, axis=0)  2.81 us
  transfers between devices with their start and end apart: 4, of which 3 were waited for; matrix products, arithmetic and copies ran while one was open for 2% of the time, Pallas kernels for 0%

commit v1 on v0

--- a/solution.py
+++ b/solution.py
@@ -1,3 +1,4 @@
+import functools
 import jax
 import jax.numpy as jnp
 from jax import lax
@@ -5,6 +6,14 @@
 
 SWEEPS = 4
 diffusion = 0.4
+
+
+def plane_load(block_in, axis_tag):
+    row_out = jax.lax.all_gather(block_in, axis_tag)
+    return jnp.sum(row_out, 0)
+
+
+pairs_all_play = functools.partial(plane_load, axis_tag="mem")
 
 
 def padded_2(block, sides, width):
@@ -77,7 +86,7 @@
     members = perturb.shape[0] * lax.axis_size("mem")
     scale = (members - 1) ** (-0.5)
     owned = partial_sum.shape[0] // lax.axis_size("mem")
-    whole_cols = lax.psum(partial_sum, "mem") * scale
+    whole_cols = pairs_all_play(partial_sum) * scale
     increment = lax.dynamic_slice_in_dim(whole_cols, lax.axis_index("mem") * owned, owned, 0)
     indices = obs_column.reshape(-1)
     background = obs_background.reshape(indices.shape[0], -1)

time: 136 us -> 106 us (0.78)
  waiting for transfers between devices: 87.5 us -> 58.5 us
    psum x1 -> x0, waiting for transfers between devices: 52.6 us -> none  [per_device(): whole_cols = lax.psum(partial_sum, 'mem') * scale]
    all_gather x0 -> x1, waiting for transfers between devices: none -> 21 us  [plane_load(): row_out = jax.lax.all_gather(block_in, axis_tag)]
    ppermute x1, waiting for transfers between devices: 2.37 us -> 4.09 us  [padded_2(): lax.ppermute(lax.slice_in_dim(block, block.shape[dim] - width, None, axis...]
    unnamed x16 -> x18, local copies, waits for them, and re-layouts: 3.27 us -> 3.27 us
  transfers between devices with their start and end apart: 4 -> 4, of which waited for: 3 -> 4; matrix products, arithmetic and copies ran while one was open for 2% -> 2% of each run, Pallas kernels for 0% -> 0%
where the time goes in v1:
time: 106 us
  waiting for transfers between devices  58.5 us (55%)
  matrix products  15.2 us (14%)
  between operations  14.9 us (14%)
  local copies, waits for them, and re-layouts  7.54 us (7%)
  starting transfers between devices  5.2 us (5%)
  other arithmetic  4.55 us (4%)
    reduce_scatter x1, waiting for transfers between devices, per_device(): lax.psum_scatter(gradient, 'mem', scatter_dimension=0, tiled=True)  33.1 us
    all_gather x1, waiting for transfers between devices, plane_load(): row_out = jax.lax.all_gather(block_in, axis_tag)  21 us
    dot_general x1, matrix products, observe_block(): lax.dot_general(back_pre, w_in, (((1,), (1,)), ((), ())), preferred_eleme...  9.44 us
    ppermute x1, starting transfers between devices, padded_2(): lax.ppermute(lax.slice_in_dim(block, 0, width, axis=dim), axis, backward)  5.12 us
    ppermute x1, waiting for transfers between devices, padded_2(): lax.ppermute(lax.slice_in_dim(block, block.shape[dim] - width, None, axis...  4.09 us
    unnamed x18, local copies, waits for them, and re-layouts  3.27 us
    dot_general x1, matrix products, observe_block(): outputs = jnp.dot(hidden_low, w_out, preferred_element_type=jnp.float32)  3.19 us
    gather x1, local copies, waits for them, and re-layouts, observe_block(): sampled = jnp.take(whole_cols, indices, axis=0)  2.81 us
  transfers between devices with their start and end apart: 4, of which 4 were waited for; matrix products, arithmetic and copies ran while one was open for 2% of the time, Pallas kernels for 0%

profile of v1, /device:TPU:0, one launch (start us, length us, event | category | flops | bytes accessed | tf_op | source)
XLA Modules:
  0.0 105.9 jit_solution(10038672683572871830)
XLA Ops:
  7.2 0.0 copy-start
  7.2 0.0 all-gather.3.cloned.1.call-start
  7.2 0.8 fusion.48
  8.1 5.1 %collective-permute-start.1 = (f32[8,4,128]{2,1,0:T(4,128)S(1)}, f32[8,4,128]{2,1,0:T(4,128)S(1)}, u32[]{:S(2)}, u32[]{:S(2)}) collective-permute-start(f32[8,4,128]{2,1,0:T(4,128)S(1)} %get-tuple-element.3), channel_id=1, source_target_pairs={{1,0},{2,1},{3,2},{0,3},{5,4},{6,5},{7,6},{4,7},{9,8},{10,9},{11,1... | collective-permute-start | bytes 49160 | tf_op jit(solution)/shard_map/ppermute | solution.py:28
  13.2 0.0 collective-permute-start
  13.2 1.1 %convert_element_type.35 = f32[8,256,128]{2,1,0:T(8,128)S(1)} convert(bf16[8,256,128]{2,1,0:T(8,128)(2,1)} %param.10) | non-fusion elementwise | flops 262144 | bytes 1572864 | tf_op jit(solution)/shard_map/convert_element_type | solution.py:80
  14.3 0.3 collective-permute-done.1
  14.6 4.1 %collective-permute-done = f32[8,4,128]{2,1,0:T(4,128)S(1)} collective-permute-done((f32[8,4,128]{2,1,0:T(4,128)S(1)}, f32[8,4,128]{2,1,0:T(4,128)S(1)}, u32[]{:S(2)}, u32[]{:S(2)}) %collective-permute-start) | collective-permute-done | bytes 16416 | tf_op jit(solution)/shard_map/ppermute | solution.py:25
  18.7 0.1 pad_maximum_fusion
  18.8 0.0 copy-start.4
  18.8 0.0 copy-start.5
  18.8 0.3 fusion.23
  19.2 0.0 copy-start.2
  19.2 0.3 fusion.21
  19.5 0.3 fusion.19
  19.8 1.1 %fusion.27 = f32[256,128]{1,0:T(8,128)} fusion(f32[8,258,128]{2,1,0:T(8,128)S(1)} %fusion.19, bf16[8,256,128]{2,1,0:T(8,128)(2,1)S(1)} %copy-done.3), kind=kLoop, calls=%fused_computation.35 | loop fusion | flops 2064384 | bytes 3801088 | tf_op jit(solution)/shard_map/reduce_sum | solution.py:85
  20.9 0.0 all-gather.3.cloned.1.call-update
  20.9 0.0 reduce-scatter.2.cloned.1.call-start
  21.7 21.0 %all-gather.3.cloned.1.call-done = f32[2048,128]{1,0:T(8,128)} async-done(((f32[256,128]{1,0:T(8,128)}), f32[2048,128]{1,0:T(8,128)}) %all-gather.3.cloned.1.call-update) | async-done | bytes 1048592 | tf_op jit(solution)/shard_map/all_gather | solution.py:12
  42.7 1.3 %reduce_sum.19 = f32[256,128]{1,0:T(8,128)S(1)} reduce(f32[8,256,128]{2,1,0:T(8,128)} %bitcast.23, f32[]{:T(128)} %constant.19.clone.1), dimensions={0}, to_apply=%region_1.0 | reduce | flops 229376 | bytes 1179652 | tf_op jit(solution)/shard_map/reduce_sum | solution.py:13
  44.0 0.0 copy-start.6
  44.0 0.0 copy-start.7
  44.0 0.0 copy-start.8
  44.0 2.8 %gather_fusion = f32[1024,128]{1,0:T(8,128)S(1)} fusion(f32[256,128]{1,0:T(8,128)S(1)} %broadcast_multiply_fusion, s32[1024]{0:T(1024)S(1)} %broadcast_clamp_fusion), kind=kCustom, calls=%fused_computation | custom fusion | bytes 1052672 | tf_op jit(solution)/shard_map/jit(_take)/gather | solution.py:43
  46.9 1.3 %fusion.31 = f32[1024,2048]{1,0:T(8,128)S(1)} fusion(bf16[128,2048]{1,0:T(8,128)(2,1)S(1)} %copy-done, f32[1024,128]{1,0:T(8,128)S(1)} %gather_fusion, bf16[1,1,1024,128]{3,2,1,0:T(8,128)(2,1)S(1)} %copy-done.2, pred[1024]{0:T(1024)(128)(4,1)S(1)} %compare_and_fusion), kind=kOutput, calls=%fused_computation.42 | convolution fusion | flops 537395200 | bytes 9700352 | tf_op jit(solution)/shard_map/dot_general | solution.py:45
  48.2 3.2 %copy-done.1 = f32[1024,2048]{1,0:T(8,128)} copy-done((f32[1024,2048]{1,0:T(8,128)}, f32[1024,2048]{1,0:T(8,128)S(1)}, u32[]{:S(2)}) %copy-start.1) | copy-done | bytes 8388632
  51.4 3.2 %fusion.14 = bf16[1024,128]{1,0:T(8,128)(2,1)S(1)} fusion(bf16[2048,128]{1,0:T(8,128)(2,1)S(1)} %copy-done.6, f32[1024,2048]{1,0:T(8,128)S(1)} %fusion.31, f32[2048]{0:T(1024)S(1)} %copy-done.8, bf16[1,1,1024,128]{3,2,1,0:T(8,128)(2,1)S(1)} %copy-done.7, f32[1024]{0:T(1024)S(1)} %fusion.36), kind=kOutput, calls=%fused_computation.16 | convolution fusion | flops 558366720 | bytes 9449472 | tf_op jit(solution)/shard_map/dot_general | solution.py:48
  54.6 9.4 %fusion.15 = bf16[1024,128]{1,0:T(8,128)(2,1)S(1)} fusion(bf16[128,2048]{1,0:T(8,128)(2,1)S(1)} %copy-done, f32[1024,2048]{1,0:T(8,128)} %copy-done.1, f32[2048]{0:T(1024)S(1)} %copy-done.8, bf16[1024,128]{1,0:T(8,128)(2,1)S(1)} %fusion.14, bf16[2048,128]{1,0:T(8,128)(2,1)S(1)} %copy-done.6), kind=kOutput, calls=%fused_computation.17 | convolution fusion | flops 1117913088 | bytes 9969664 | tf_op jit(solution)/shard_map/dot_general | solution.py:57
  64.0 1.3 %fusion.28 = f32[256,128]{1,0:T(8,128)} fusion(bf16[1024,128]{1,0:T(8,128)(2,1)S(1)} %fusion.15, s32[1024]{0:T(1024)S(1)} %bitcast.25), kind=kOutput, calls=%fused_computation.38 | convolution fusion | flops 67371008 | bytes 397312 | tf_op jit(solution)/shard_map/dot_general | solution.py:63
  65.3 0.0 reduce-scatter.2.cloned.1.call-update
  65.3 0.6 constant_dynamic-slice_fusion
  66.0 33.1 %reduce-scatter.2.cloned.1.call-done = f32[32,128]{1,0:T(8,128)} async-done(((f32[256,128]{1,0:T(8,128)}), f32[32,128]{1,0:T(8,128)}) %reduce-scatter.2.cloned.1.call-update) | async-done | bytes 16400 | tf_op jit(solution)/shard_map/reduce_scatter | solution.py:101
  (15 shorter events, 0.1 us)
Async XLA Ops:
  7.2 39.7 %copy-start = (bf16[128,2048]{1,0:T(8,128)(2,1)S(1)}, bf16[128,2048]{1,0:T(8,128)(2,1)}, u32[]{:S(2)}) copy-start(bf16[128,2048]{1,0:T(8,128)(2,1)} %param.17) | copy-start | bytes 1572868
  7.2 12.6 %copy-start.3 = (bf16[8,256,128]{2,1,0:T(8,128)(2,1)S(1)}, bf16[8,256,128]{2,1,0:T(8,128)(2,1)}, u32[]{:S(2)}) copy-start(bf16[8,256,128]{2,1,0:T(8,128)(2,1)} %param.11) | copy-start | bytes 1572868
  7.2 35.5 %all-gather.3.cloned.1.call-start = ((), (), s32[]{:S(2)}) async-start(), calls=%async_computation.2 | async-start | bytes 1179648 | tf_op jit(solution)/shard_map/all_gather | solution.py:12
  8.1 6.6 %collective-permute-start.1 = (f32[8,4,128]{2,1,0:T(4,128)S(1)}, f32[8,4,128]{2,1,0:T(4,128)S(1)}, u32[]{:S(2)}, u32[]{:S(2)}) collective-permute-start(f32[8,4,128]{2,1,0:T(4,128)S(1)} %get-tuple-element.3), channel_id=1, source_target_pairs={{1,0},{2,1},{3,2},{0,3},{5,4},{6,5},{7,6},{4,7},{9,8},{10,9},{11,1... | collective-permute-start | bytes 49160 | tf_op jit(solution)/shard_map/ppermute | solution.py:28
  13.2 5.5 %collective-permute-start = (f32[8,4,128]{2,1,0:T(4,128)S(1)}, f32[8,4,128]{2,1,0:T(4,128)S(1)}, u32[]{:S(2)}, u32[]{:S(2)}) collective-permute-start(f32[8,4,128]{2,1,0:T(4,128)S(1)} %get-tuple-element.2), channel_id=1, source_target_pairs={{0,1},{1,2},{2,3},{3,0},{4,5},{5,6},{6,7},{7,4},{8,9},{9,10},{10,1... | collective-permute-start | bytes 49160 | tf_op jit(solution)/shard_map/ppermute | solution.py:25
  18.8 2.8 %copy-start.4 = (s32[1,1,1024]{2,1,0:T(1,128)S(1)}, s32[1,1,1024]{2,1,0:T(1,128)}, u32[]{:S(2)}) copy-start(s32[1,1,1024]{2,1,0:T(1,128)} %param.12) | copy-start | bytes 12292
  18.8 2.9 %copy-start.5 = (f32[1,1,1024]{2,1,0:T(1,128)S(1)}, f32[1,1,1024]{2,1,0:T(1,128)}, u32[]{:S(2)}) copy-start(f32[1,1,1024]{2,1,0:T(1,128)} %param.16) | copy-start | bytes 12292
  19.2 27.7 %copy-start.2 = (bf16[1,1,1024,128]{3,2,1,0:T(8,128)(2,1)S(1)}, bf16[1,1,1024,128]{3,2,1,0:T(8,128)(2,1)}, u32[]{:S(2)}) copy-start(bf16[1,1,1024,128]{3,2,1,0:T(8,128)(2,1)} %param.14) | copy-start | bytes 786436
  20.9 78.1 %reduce-scatter.2.cloned.1.call-start = ((), (), s32[]{:S(2)}) async-start(), calls=%async_computation.1 | async-start | bytes 147456 | tf_op jit(solution)/shard_map/reduce_scatter | solution.py:101
  44.0 7.4 %copy-start.6 = (bf16[2048,128]{1,0:T(8,128)(2,1)S(1)}, bf16[2048,128]{1,0:T(8,128)(2,1)}, u32[]{:S(2)}) copy-start(bf16[2048,128]{1,0:T(8,128)(2,1)} %param.19) | copy-start | bytes 1572868
  44.0 7.4 %copy-start.7 = (bf16[1,1,1024,128]{3,2,1,0:T(8,128)(2,1)S(1)}, bf16[1,1,1024,128]{3,2,1,0:T(8,128)(2,1)}, u32[]{:S(2)}) copy-start(bf16[1,1,1024,128]{3,2,1,0:T(8,128)(2,1)} %param.15) | copy-start | bytes 786436
  44.0 7.4 %copy-start.8 = (f32[2048]{0:T(1024)S(1)}, f32[2048]{0:T(1024)}, u32[]{:S(2)}) copy-start(f32[2048]{0:T(1024)} %param.18) | copy-start | bytes 24580
  48.2 3.2 %copy-start.1 = (f32[1024,2048]{1,0:T(8,128)}, f32[1024,2048]{1,0:T(8,128)S(1)}, u32[]{:S(2)}) copy-start(f32[1024,2048]{1,0:T(8,128)S(1)} %fusion.31) | copy-start | bytes 25165828
Sparse Core Ops, SparseCore 0:
  21.1 21.5 all-gather.2
  65.5 33.5 reduce-scatter.1
